TPU v7x, 512 devices: a 4x2x32 block of a 4x8x32 slice. The times are simulated.
512 devices in a mesh: groups: 2 (over y), seq: 32 (over z), head: 4 (over x), sub: 2 (over core).
Axes of the slice: x: 4, y: 2, z: 32, core: 2. Of those that a mesh axis runs over, the one named last changes fastest.
The devices are a block of a 4x8x32 slice.
Arguments:
- hidden: bfloat16 [8192, 7168], P(('groups', 'seq')), parts along dimension 0, may hold values from -240 to 240
- segment_ids: int32 [8192], P('groups'), parts along dimension 0, may hold values from 0 to 2, never falling along the last dimension, each value on 1 to 2048 neighbouring positions
- attn_gain: float32 [7168], replicated, may hold values from 0.1 to 1.9
- down_weight: bfloat16 [7168, 2112], P('seq', ('head', 'sub')), may hold values from -0.0625 to 0.0625
- q_gain: float32 [1536], replicated, may hold values from 0.1 to 1.9
- kv_gain: float32 [512], replicated, may hold values from 0.1 to 1.9
- q_up: bfloat16 [1536, 12288], P('seq', ('head', 'sub')), may hold values from -0.15625 to 0.15625
- key_up: bfloat16 [8192, 512], P(('head', 'sub'), 'seq'), may hold values from -8 to 8
- value_up: bfloat16 [512, 8192], P('seq', ('head', 'sub')), may hold values from -1 to 1
Outputs:
- attended: bfloat16 [8192, 8192], P(('groups', 'seq'), ('head', 'sub')), parts along dimension 0
There are 2 independent parts, one for each index of `groups`. A program takes and returns all parts, laid end to end along the dimension named above; an argument that names none is the same for every part. Nothing has to cross between parts.
Inputs may be any that keep to these rules, and one draw needn't show every extreme that they name: `segment_ids`: document numbers never fall along the pack.
All inputs are finite; a program needn't handle non-finite values.
Results may differ from a plain program's by a relative error of at most 0.014.
The roundings to bfloat16 on the way count: a program that leaves them out, or rounds other values in their place, can miss the bound.
Values may be sent and summed in bfloat16 or wider, within the bound.
A program may use at most 64 MiB of HBM per device.

v0:
```python
import functools
import math

import jax
import jax.numpy as jnp
from jax import lax
from jax.sharding import PartitionSpec as P

QL = 1536
KVL = 512
ROPE = 64
NOPE = 128
VDIM = 128


EPSILON = 1e-06
ROPE_BASE = 10000.0
LOWEST_SCORE = -1e30


def laid_out(pieces, dim):
    shape = list(pieces.shape[1:])
    shape[dim] *= pieces.shape[0]
    return jnp.moveaxis(pieces, 0, dim).reshape(shape)


def from_everyone(value, axis):
    copies = jnp.broadcast_to(value, (lax.axis_size(axis), *value.shape))
    return lax.all_to_all(copies, axis, split_axis=0, concat_axis=0, tiled=True)


def gathered_copies(value, axis, dim):
    return laid_out(from_everyone(value, axis), dim)


def rotate(values, positions):
    half_width = values.shape[-1] // 2
    frequency = ROPE_BASE ** (-jnp.arange(half_width, dtype=jnp.float32) / half_width)
    angles = positions.astype(jnp.float32)[:, None] * frequency[None, :]
    target_shape = (angles.shape[0],) + (1,) * (values.ndim - 2) + (half_width,)
    cosine = jnp.cos(angles).reshape(target_shape)
    sine_part = jnp.sin(angles).reshape(target_shape)
    leading = values[..., :half_width]
    second = values[..., half_width:]
    return jnp.concatenate(
        [leading * cosine - second * sine_part, leading * sine_part + second * cosine], axis=-1
    )


def rms_scale(values):
    return lax.rsqrt(jnp.mean(values * values, axis=-1, keepdims=True) + EPSILON)


def make_keys(columns, positions, kv_gain):
    latent_raw = columns[:, :KVL].astype(jnp.float32)
    latent = (latent_raw * rms_scale(latent_raw) * kv_gain[None, :]).astype(jnp.bfloat16)
    key_rope = rotate(columns[:, KVL:].astype(jnp.float32), positions).astype(jnp.bfloat16)
    return jnp.concatenate([latent, key_rope], axis=1)


def unchanged(carry_state):
    return carry_state


def local(hidden, segment_ids, attn_gain, down_weight, q_gain, kv_gain, q_up, key_up, value_up):
    row_count = hidden.shape[0]
    half_rows = row_count // 2
    cycle_index = lax.axis_index("seq")
    positions = cycle_index * row_count + jnp.arange(row_count, dtype=jnp.int32)
    own_segments = jnp.take(segment_ids, positions)
    widened = hidden.astype(jnp.float32)
    inverse = rms_scale(widened)
    scaled = (widened * attn_gain[None, :]).astype(jnp.bfloat16)
    chosen = scaled
    down_part = jnp.dot(
        chosen,
        lax.all_gather(down_weight, "seq", axis=0, tiled=True),
        preferred_element_type=jnp.float32,
    )
    down_part = (down_part * inverse).astype(jnp.bfloat16)
    projected = lax.all_gather(down_part, ("head", "sub"), axis=1, tiled=True)
    query_low = projected[:, :QL].astype(jnp.float32)
    query_latent = (query_low * rms_scale(query_low) * q_gain[None, :]).astype(jnp.bfloat16)
    head_count = q_up.shape[1] // (NOPE + ROPE)
    chosen = query_latent
    query_full = jnp.dot(
        chosen, lax.all_gather(q_up, "seq", axis=0, tiled=True), preferred_element_type=jnp.float32
    )
    query_full = query_full.astype(jnp.bfloat16).reshape(row_count, head_count, NOPE + ROPE)
    query_rope = rotate(query_full[:, :, NOPE:].astype(jnp.float32), positions).astype(jnp.bfloat16)
    query_nope = query_full[:, :, :NOPE]
    shard_piece = gathered_copies(key_up, "seq", 1)
    blocks = shard_piece.reshape(head_count, NOPE, shard_piece.shape[1])
    absorbed = jnp.einsum(
        "thc,hcn->thn", query_nope, blocks, preferred_element_type=jnp.float32
    ).astype(jnp.bfloat16)
    queries = jnp.concatenate([absorbed, query_rope], axis=2)
    score_scale = (NOPE + ROPE) ** (-0.5)
    halves = (queries[:half_rows], queries[half_rows:])
    half_pos = (positions[:half_rows], positions[half_rows:])
    half_seg = (own_segments[:half_rows], own_segments[half_rows:])

    def attend(carry_state, key_block, key_pos, key_seg, half_index):
        running_max, running_sum, accumulator = carry_state
        scores = (
            jnp.einsum(
                "thc,nc->htn", halves[half_index], key_block, preferred_element_type=jnp.float32
            )
            * score_scale
        )
        allowed = (key_pos[None, :] <= half_pos[half_index][:, None]) & (
            key_seg[None, :] == half_seg[half_index][:, None]
        )
        scores = jnp.where(allowed[None], scores, -jnp.inf)
        new_max = jnp.maximum(running_max, jnp.max(scores, axis=2))
        shrink = jnp.exp(running_max - new_max)
        weights = jnp.exp(scores - new_max[:, :, None])
        running_sum = running_sum * shrink + jnp.sum(weights, axis=2)
        accumulator = accumulator * shrink[:, :, None] + jnp.einsum(
            "htn,nc->htc",
            weights.astype(jnp.bfloat16),
            key_block[:, :KVL],
            preferred_element_type=jnp.float32,
        )
        return (new_max, running_sum, accumulator)

    start_state = tuple(
        (
            (
                jnp.full((head_count, half_rows), LOWEST_SCORE, jnp.float32),
                jnp.zeros((head_count, half_rows), jnp.float32),
                jnp.zeros((head_count, half_rows, KVL), jnp.float32),
            )
            for half_index in range(2)
        )
    )
    share_count = lax.axis_size(("head", "sub"))
    share_rows = row_count // share_count
    share_first = lax.axis_index(("head", "sub")) * share_rows
    own_columns = lax.dynamic_slice_in_dim(projected[:, QL:], share_first, share_rows, 0)
    own_positions = lax.dynamic_slice_in_dim(positions, share_first, share_rows, 0)
    own_keys = make_keys(own_columns, own_positions, kv_gain)
    shard_piece = gathered_copies(own_keys, "seq", 0)
    shard_total = shard_piece.shape[0] // share_rows
    stacked = shard_piece.reshape(shard_total, share_rows, shard_piece.shape[1])
    assembled = gathered_copies(stacked, ("head", "sub"), 1)
    assembled = assembled.reshape(shard_total * row_count, shard_piece.shape[1])
    piece_rows = assembled.shape[0]
    block_rows = math.gcd(piece_rows, row_count)
    blocks = assembled.reshape(piece_rows // block_rows, block_rows, assembled.shape[1])
    firsts = block_rows * jnp.arange(piece_rows // block_rows, dtype=jnp.int32)

    def visit_block(block_state, scan_item):
        key_block, block_start = scan_item
        key_pos = block_start + jnp.arange(block_rows, dtype=jnp.int32)
        key_seg = jnp.take(segment_ids, key_pos)
        updated = []
        for half_index in range(2):
            is_live = jnp.min(key_pos) <= jnp.max(half_pos[half_index])
            refresh = functools.partial(
                attend, key_block=key_block, key_pos=key_pos, key_seg=key_seg, half_index=half_index
            )
            updated.append(lax.cond(is_live, refresh, unchanged, block_state[half_index]))
        return (tuple(updated), None)

    final_state, unused = lax.scan(visit_block, start_state, (blocks, firsts))
    attended = jnp.concatenate(
        [
            (accumulator / running_sum[:, :, None]).astype(jnp.bfloat16)
            for running_max, running_sum, accumulator in final_state
        ],
        axis=1,
    )
    shard_piece = gathered_copies(value_up, "seq", 0)
    chosen = attended
    blocks = shard_piece.reshape(shard_piece.shape[0], head_count, VDIM)
    result = jnp.einsum("htn,nhv->thv", chosen, blocks, preferred_element_type=jnp.float32)
    result = result.reshape(row_count, head_count * VDIM).astype(jnp.bfloat16)
    return result


def solution(mesh):
    placed = (
        P(("groups", "seq"), None),
        P("groups"),
        P(),
        P("seq", ("head", "sub")),
        P(),
        P(),
        P("seq", ("head", "sub")),
        P(("head", "sub"), "seq"),
        P("seq", ("head", "sub")),
    )
    return jax.shard_map(
        local,
        mesh=mesh,
        in_specs=placed,
        out_specs=P(("groups", "seq"), ("head", "sub")),
        check_vma=False,
    )
```

profile of v0, /device:TPU:1952, one launch (start us, length us, event | category | flops | bytes accessed | tf_op | source)
XLA Modules:
  0.0 853.1 jit_solution(4573938176594299014)
XLA Ops:
  8.4 6.5 all-to-all-start.2
  15.7 113.6 %all-to-all-done.2 = bf16[32,1024,16]{1,2,0:T(8,128)(2,1)S(1)} async-done(((bf16[32,1024,16]{1,2,0:T(8,128)(2,1)}), bf16[32,1024,16]{1,2,0:T(8,128)(2,1)S(1)}, u32[]{:S(2)}, u32[]{:S(2)}) %all-to-all-start.2) | async-done | bytes 1048608 | tf_op jit(solution)/shard_map/all_to_all | solution.py:29
  130.4 6.3 all-to-all-start.3
  137.6 1.9 fusion.20
  139.6 142.9 %all-gather.6.cloned.1.call-done = bf16[32,224,264]{1,2,0:T(8,128)(2,1)} async-done(((bf16[1,224,264]{1,2,0:T(8,128)(2,1)}), bf16[32,224,264]{1,2,0:T(8,128)(2,1)}) %all-gather.6.cloned.1.call-update) | async-done | bytes 3784720 | tf_op jit(solution)/shard_map/all_gather | solution.py:77
  282.5 5.3 copy.70
  287.8 9.1 %reshape.234 = bf16[7168,264]{0,1:T(8,128)(2,1)} reshape(bf16[32,224,264]{1,0,2:T(8,128)(2,1)} %copy.70) | data formatting | bytes 7569408
  296.9 3.8 fusion.28
  300.7 13.6 %all_gather.10 = bf16[128,2112]{0,1:T(8,128)(2,1)S(1)} all-gather(bf16[128,264]{0,1:T(8,128)(2,1)S(1)} %fusion.28), channel_id=1, replica_groups=mesh['groups'=2,'seq'=32,'head'=4,'sub'=2] {'head','sub'}, dimensions={1}, use_global_device_ids=true | all-gather | bytes 608256 | tf_op jit(solution)/shard_map/all_gather | solution.py:81
  315.2 94.7 %all_to_all.20 = bf16[32,16,576]{2,1,0:T(8,128)(2,1)S(1)} all-to-all(bf16[32,16,576]{2,1,0:T(8,128)(2,1)S(1)} %broadcast_in_dim.41), channel_id=1, replica_groups=mesh['groups'=2,'seq'=32,'head'=4,'sub'=2] {'seq'}, dimensions={0} | all-to-all | bytes 1179648 | tf_op jit(solution)/shard_map/all_to_all | solution.py:29
  410.0 2.7 broadcast_in_dim.42
  412.7 5.2 all-to-all-start.1
  422.0 44.1 %all-gather.4.cloned.1.call-done = bf16[1536,1536]{1,0:T(8,128)(2,1)} async-done(((bf16[48,1536]{1,0:T(8,128)(2,1)}), bf16[1536,1536]{1,0:T(8,128)(2,1)}) %all-gather.4.cloned.1.call-update) | async-done | bytes 4718608 | tf_op jit(solution)/shard_map/all_gather | solution.py:87
  466.1 3.4 convolution_convert_fusion
  472.0 6.5 all-to-all-done.1
  478.5 5.6 copy.72
  484.4 359.2 %while.21 = (s32[]{:T(128)}, f32[8,64]{1,0:T(8,128)S(1)}, f32[8,64]{1,0:T(8,128)S(1)}, f32[8,64,512]{2,1,0:T(8,128)S(1)}, f32[8,64]{1,0:T(8,128)S(1)}, /*index=5...) while((s32[]{:T(128)}, f32[8,64]{1,0:T(8,128)S(1)}, ...), condition=%wide.region_15.17_spmd, body=%wide.region_5.16_spmd.sunk | while | flops 287232768 | bytes 7917033 | solution.py:166
  493.3 2.4 conditional.4
  504.6 2.4 conditional.4
  516.0 2.4 conditional.4
  527.3 2.4 conditional.4
  538.6 2.4 conditional.4
  550.0 2.4 conditional.4
  561.3 2.4 conditional.4
  572.7 2.4 conditional.4
  584.0 2.4 conditional.4
  595.4 2.4 conditional.4
  606.7 2.4 conditional.4
  618.0 2.4 conditional.4
  629.4 2.4 conditional.4
  640.7 2.4 conditional.4
  652.1 2.4 conditional.4
  663.4 2.4 conditional.4
  674.8 2.4 conditional.4
  686.1 2.4 conditional.4
  697.4 2.4 conditional.4
  708.8 2.4 conditional.4
  720.1 2.4 conditional.4
  731.5 2.4 conditional.4
  742.8 2.4 conditional.4
  754.2 2.4 conditional.4
  765.5 2.4 conditional.4
  776.8 2.4 conditional.4
  788.2 2.4 conditional.4
  799.5 2.4 conditional.4
  810.9 2.4 conditional.4
  822.2 2.4 conditional.4
  833.6 2.4 conditional.4
  (758 shorter events, 330.6 us)
Async XLA Ops:
  6.5 122.7 %copy-start.3 = (bf16[16,1024]{1,0:T(8,128)(2,1)S(1)}, bf16[16,1024]{1,0:T(8,128)(2,1)}, u32[]{:S(2)}) copy-start(bf16[16,1024]{1,0:T(8,128)(2,1)} %param.25) | copy-start | bytes 98308
  8.4 120.8 %all-to-all-start.2 = ((bf16[32,1024,16]{1,2,0:T(8,128)(2,1)}), bf16[32,1024,16]{1,2,0:T(8,128)(2,1)S(1)}, u32[]{:S(2)}, u32[]{:S(2)}) async-start(bf16[32,1024,16]{1,2,0:T(8,128)(2,1)} %broadcast_in_dim.43), calls=%async_computation.2 | async-start | bytes 2097152 | tf_op jit(solution)/shard_map/all_to_all | solution.py:29
  14.9 267.6 %all-gather.6.cloned.1.call-start = ((), (), s32[]{:S(2)}) async-start(), calls=%async_computation.5 | async-start | bytes 4460544 | tf_op jit(solution)/shard_map/all_gather | solution.py:77
  130.4 184.7 %all-to-all-start.3 = ((bf16[32,16,1024]{2,1,0:T(8,128)(2,1)}), bf16[32,16,1024]{2,1,0:T(8,128)(2,1)S(1)}, u32[]{:S(2)}, u32[]{:S(2)}) async-start(bf16[32,16,1024]{2,1,0:T(8,128)(2,1)} %broadcast_in_dim.44), calls=%async_computation.3 | async-start | bytes 2097152 | tf_op jit(solution)/shard_map/all_to_all | solution.py:29
  136.7 329.4 %all-gather.4.cloned.1.call-start = ((), (), s32[]{:S(2)}) async-start(), calls=%async_computation.4 | async-start | bytes 4866048 | tf_op jit(solution)/shard_map/all_gather | solution.py:87
  287.8 9.1 %copy-start.6 = (f32[7168]{0:T(1024)S(1)}, f32[7168]{0:T(1024)}, u32[]{:S(2)}) copy-start(f32[7168]{0:T(1024)} %param.19) | copy-start | bytes 86020
  296.9 18.1 %copy-start.5 = (f32[512]{0:T(512)S(1)}, f32[512]{0:T(512)}, u32[]{:S(2)}) copy-start(f32[512]{0:T(512)} %param.22) | copy-start | bytes 6148
  314.4 105.9 %copy-start.1 = (bf16[128,2112]{0,1:T(8,128)(2,1)}, bf16[128,2112]{0,1:T(8,128)(2,1)S(1)}, u32[]{:S(2)}) copy-start(bf16[128,2112]{0,1:T(8,128)(2,1)S(1)} %all_gather.10) | copy-start | bytes 1622020
  412.7 5.2 copy-start
  412.7 65.8 %all-to-all-start.1 = ((bf16[8,32,16,576]{3,2,1,0:T(8,128)(2,1)}), bf16[8,32,16,576]{3,2,1,0:T(8,128)(2,1)}, u32[]{:S(2)}, u32[]{:S(2)}) async-start(bf16[8,32,16,576]{3,2,1,0:T(8,128)(2,1)} %broadcast_in_dim.42), calls=%async_computation.1 | async-start | bytes 10485760 | tf_op jit(solution)/shard_map/all_to_all | solution.py:29
  417.9 48.2 %copy-start.4 = (f32[1536]{0:T(1024)S(1)}, f32[1536]{0:T(1024)}, u32[]{:S(2)}) copy-start(f32[1536]{0:T(1024)} %param.21) | copy-start | bytes 18436
  843.6 1.2 copy-start.2
Sparse Core Ops, SparseCore 0:
  17.8 264.6 all-gather.5
  284.6 181.5 all-gather.3
where the time goes:
time: 859 us; the launch traced here: 853 us
  waiting for transfers between devices  309 us (36%)
  local copies, waits for them, and re-layouts  118 us (14%)
  blocking collectives  108 us (13%)
  other arithmetic  104 us (12%)
  matrix products  97.9 us (11%)
  loops' own time  85.1 us (10%)
  starting transfers between devices  18 us (2%)
  between operations  13.8 us (2%)
    all_gather x1, waiting for transfers between devices, local(): lax.all_gather(down_weight, 'seq', axis=0, tiled=True)  143 us
    all_to_all x3, waiting for transfers between devices, from_everyone(): return lax.all_to_all(copies, axis, split_axis=0, concat_axis=0, tiled=True)  120 us
    all_to_all x1, blocking collectives, from_everyone(): return lax.all_to_all(copies, axis, split_axis=0, concat_axis=0, tiled=True)  94.7 us
    another operation x1, loops' own time, local(): final_state, unused = lax.scan(visit_block, start_state, (blocks, firsts))  81.2 us
    dot_general x62, matrix products, attend(): jnp.einsum('thc,nc->htn', halves[half_index], key_block, preferred_elemen...  59.4 us
    all_gather x1, waiting for transfers between devices, local(): lax.all_gather(q_up, 'seq', axis=0, tiled=True)  44.1 us
    reduce_min x32, other arithmetic, visit_block(): is_live = jnp.min(key_pos) <= jnp.max(half_pos[half_index])  39.4 us
    gather x32, local copies, waits for them, and re-layouts, visit_block(): key_seg = jnp.take(segment_ids, key_pos)  36.7 us
  transfers between devices with their start and end apart: 5, of which 4 were waited for; matrix products, arithmetic and copies ran while one was open for 4% of the time, Pallas kernels for 0%

commit v1 on v0

v1 whole, which is shorter than its diff:
```python
import functools
import math

import jax
import jax.numpy as jnp
from jax import lax
from jax.experimental import pallas as pl
from jax.experimental.pallas import tpu as pltpu
from jax.sharding import PartitionSpec as P

QL = 1536
KVL = 512
ROPE = 64
NOPE = 128
VDIM = 128
LONGEST = 2048
LANES = 128
EPSILON = 1e-06
ROPE_BASE = 10000.0
BF16 = jnp.bfloat16
F32 = jnp.float32
MESH = pl.DeviceIdType.MESH


def nt_dot(a, b):
    return lax.dot_general(a, b, (((1,), (1,)), ((), ())), preferred_element_type=F32)


def kernel(
    cfg,
    hid, gain, dpk, qpk, kpk, vpk, q_gain, kv_gain, cosine, sine, first,
    out,
    sc, g_d, g_q, g_k, g_v, p_all, down, kb, kbt, qb, bias, ql, query, s_buf,
    acc, acc_tail, sumsq, total,
    send_sem, recv_sem, p_send, p_recv, z_send, z_recv, x_send, x_recv,
):
    n, n_sub, plane = cfg["n"], cfg["n_sub"], cfg["plane"]
    rows, feat, main = cfg["rows"], cfg["feat"], cfg["main"]
    back, heads = cfg["back"], cfg["heads"]
    share = rows // plane
    z = lax.axis_index("seq")
    me = lax.axis_index("head") * n_sub + lax.axis_index("sub")

    def peer(d):
        other = lax.rem(me + d, plane)
        return {"head": other // n_sub, "sub": lax.rem(other, n_sub)}

    def along(d):
        return {"seq": lax.rem(z + d + n, n)}

    jumps = sorted({1, n - 1, 4, n - 4})
    barrier = pltpu.get_barrier_semaphore()
    for d in jumps:
        pl.semaphore_signal(barrier, inc=1, device_id=along(d), device_id_type=MESH)
    for d in range(1, plane):
        pl.semaphore_signal(barrier, inc=1, device_id=peer(d), device_id_type=MESH)
    pl.semaphore_wait(barrier, len(jumps) + plane - 1)

    dr, qr, kr, vr = dpk.shape[0], qpk.shape[0], kpk.shape[0], vpk.shape[0]
    chunks = []
    pieces = dr // 48 if dr % 48 == 0 else 1
    step = dr // pieces
    for c in range(pieces):
        chunks.append((dpk, g_d, dr, c * step, step))
    chunks.append((kpk, g_k, kr, 0, kr))
    phase_one = list(range(len(chunks)))
    for c in range(3):
        chunks.append((qpk, g_q, qr, c * (qr // 3), qr // 3))
    chunks.append((vpk, g_v, vr, 0, vr))
    phase_two = list(range(len(phase_one), len(chunks)))
    hops = (n - 1 - n // 2, n // 2)
    signs = (1, -1)

    def ring_copy(c, way, step_index, origin, own=False):
        src, held, size, offset, length = chunks[c]
        at = pl.ds(pl.multiple_of(origin * size + offset, 16), length)
        return pltpu.make_async_remote_copy(
            src_ref=src.at[pl.ds(offset, length), :] if own else held.at[at, :],
            dst_ref=held.at[at, :],
            send_sem=send_sem.at[c, way],
            recv_sem=recv_sem.at[c, way, step_index],
            device_id=along(signs[way]),
            device_id_type=MESH,
        )

    def origin_of(way, s):
        return lax.rem(z - signs[way] * s + 2 * n, n)

    def ring_start(which):
        for c in which:
            for way in (0, 1):
                ring_copy(c, way, 0, z, own=True).start()

    def ring_step(which, s, ways, forward):
        for c in which:
            for way in ways:
                origin = origin_of(way, s)
                ring_copy(c, way, s - 1, origin).wait_recv()
                if way in forward:
                    ring_copy(c, way, s - 1, origin).wait_send()
                    ring_copy(c, way, s, origin).start()

    def ring_ways(s):
        ways = [w for w in (0, 1) if s <= hops[w]]
        forward = [w for w in (0, 1) if s < hops[w]]
        return ways, forward

    def ring_finish(which):
        for c in which:
            for way in (0, 1):
                ring_copy(c, way, hops[way] - 1, z).wait_send()

    ring_start(phase_one)

    lane = lax.broadcasted_iota(jnp.int32, (rows, 2 * LANES), 1)
    period = LANES // cfg["gcd"]

    def cut(group, sq):
        base = pl.multiple_of(group * (period * feat), LANES)
        for i in range(period):
            offset = i * feat
            low = offset // LANES * LANES
            shift = offset - low
            width = -(-(shift + feat) // LANES) * LANES
            wide = hid[:, pl.ds(pl.multiple_of(base + low, LANES), width)].astype(F32)
            gains = gain[:, pl.ds(pl.multiple_of(base + low, LANES), width)]
            if shift:
                wide_s = pltpu.roll(wide * gains, width - shift, axis=1)
            else:
                wide_s = wide * gains
            wide_s = wide_s[:, : 2 * LANES]
            kept = jnp.where(lane < feat, wide_s, 0.0)
            sc[group * period + i] = kept.astype(BF16)
        whole = hid[:, pl.ds(base, period * feat)].astype(F32)
        squared = whole * whole
        for t in range(period * feat // LANES):
            sq = sq + squared[:, t * LANES : (t + 1) * LANES]
        return sq

    sumsq[...] = lax.fori_loop(0, n // period, cut, jnp.zeros((rows, LANES), F32))

    acc[...] = jnp.zeros_like(acc)
    acc_tail[...] = jnp.zeros_like(acc_tail)

    def project(origin, own=False):
        lhs = sc[origin]
        if own:
            rhs, tail = dpk[pl.ds(0, feat), :], dpk[pl.ds(feat, 16), :]
        else:
            start = origin * dr
            rhs = g_d[pl.ds(pl.multiple_of(start, 16), feat), :]
            tail = g_d[pl.ds(pl.multiple_of(start + feat, 16), 16), :]
        acc[...] += jnp.dot(lhs[:, :feat], rhs, preferred_element_type=F32)
        acc_tail[...] += nt_dot(lhs, tail)

    project(z, own=True)

    both = min(hops)

    def one_step(s, carry):
        ring_step(phase_one, s, (0, 1), (0, 1))
        project(origin_of(0, s))
        project(origin_of(1, s))
        return carry

    lax.fori_loop(1, both, one_step, 0)
    g_k[pl.ds(pl.multiple_of(z * kr, 16), kr), :] = kpk[...]
    for s in range(both, max(hops) + 1):
        if s == max(hops):
            ring_start(phase_two)
        ways, forward = ring_ways(s)
        ring_step(phase_one, s, ways, forward)
        for way in ways:
            project(origin_of(way, s))
    ring_finish(phase_one)

    def unit(k):
        return kb.at[pl.ds(pl.multiple_of(k * rows + me * share, 16), share), :]

    def p_copy(d):
        return pltpu.make_async_remote_copy(
            src_ref=p_all.at[me], dst_ref=p_all.at[me], send_sem=p_send, recv_sem=p_recv,
            device_id=peer(d), device_id_type=MESH,
        )

    def send_projection():
        mean = jnp.sum(sumsq[...], axis=1, keepdims=True) / (n * feat)
        inverse = lax.rsqrt(mean + EPSILON)
        p_all[me, :, 0:main] = (acc[...] * inverse).astype(BF16)
        p_all[me, :, main : main + LANES] = jnp.zeros((rows, LANES), BF16)
        p_all[me, :, main : main + 16] = (acc_tail[...] * inverse).astype(BF16)
        for d in range(1, plane):
            p_copy(d).start()

    def rope(values):
        w = values.shape[1]
        at = lax.broadcasted_iota(jnp.int32, values.shape, 1)
        swapped = jnp.where(
            lax.rem(at, ROPE) < ROPE // 2,
            pltpu.roll(values, w - ROPE // 2, axis=1),
            pltpu.roll(values, ROPE // 2, axis=1),
        )
        return values * cosine[...] + swapped * sine[...]

    def make_bias():
        query_pos = z * rows + lax.broadcasted_iota(jnp.int32, (rows, rows), 0)
        start = jnp.broadcast_to(first[...], (rows, rows))
        for k in range(back + 1):
            key_pos = (z - k) * rows + lax.broadcasted_iota(jnp.int32, (rows, rows), 1)
            allowed = (key_pos <= query_pos) & (key_pos >= start)
            bias[:, k * rows : (k + 1) * rows] = jnp.where(allowed, 0.0, -jnp.inf)

    def gather_projection():
        several = p_all.at[pl.ds(0, plane - 1)]
        pltpu.make_async_copy(several, several, p_recv).wait()
        down[...] = jnp.zeros_like(down)
        width = main + LANES
        for j in range(plane):
            piece = p_all[j].astype(F32)
            shift = j * cfg["tail"]
            if shift:
                piece = pltpu.roll(piece, shift, axis=1)
            down[:, j * main : j * main + width] += piece
        q = down[:, 0:QL]
        scale = lax.rsqrt(jnp.mean(q * q, axis=1, keepdims=True) + EPSILON)
        ql[...] = (q * scale * q_gain[...]).astype(BF16)
        c = down[:, QL : QL + KVL]
        scale = lax.rsqrt(jnp.mean(c * c, axis=1, keepdims=True) + EPSILON)
        kb[0:rows, 0:KVL] = (c * scale * kv_gain[...]).astype(BF16)
        turned = rope(down[:, QL + KVL : QL + KVL + LANES])
        turned = turned + pltpu.roll(turned, ROPE, axis=1)
        kb[0:rows, KVL : KVL + LANES] = turned.astype(BF16)

    def z_copy(k, jump):
        return pltpu.make_async_remote_copy(
            src_ref=unit(k), dst_ref=unit(k + jump),
            send_sem=z_send.at[k + jump], recv_sem=z_recv.at[k + jump],
            device_id=along(jump), device_id_type=MESH,
        )

    def x_copy(k, d):
        return pltpu.make_async_remote_copy(
            src_ref=unit(k), dst_ref=unit(k), send_sem=x_send.at[k], recv_sem=x_recv.at[k],
            device_id=peer(d), device_id_type=MESH,
        )

    parents = {}
    ticks = {0: [0]}
    for k in range(1, back + 1):
        m, r = k // 4, k % 4
        parents[k] = 1 if r else 4
        ticks.setdefault(m + r, []).append(k)

    def x_bytes(k):
        return kb.at[pl.ds(k * rows, rows - share), :]

    def transpose_slot(k):
        for t in range(kb.shape[1] // LANES):
            tile = kb[k * rows : (k + 1) * rows, t * LANES : (t + 1) * LANES]
            kbt[t * LANES : (t + 1) * LANES, k * rows : (k + 1) * rows] = (
                tile.astype(F32).T.astype(BF16)
            )

    def tick(t):
        arrived = sorted(ticks[t], key=lambda k: k % 4)
        for k in arrived:
            if k:
                z_copy(k - parents[k], parents[k]).wait_recv()
            for jump in (4, 1):
                if k + jump <= back and parents[k + jump] == jump:
                    if jump == 4 and k % 4:
                        continue
                    z_copy(k, jump).start()
        for k in arrived:
            if k:
                for d in range(1, plane):
                    x_copy(k, d).start()

    def settle(t):
        for k in ticks[t]:
            if k:
                pltpu.make_async_copy(x_bytes(k), x_bytes(k), x_recv.at[k]).wait()
            transpose_slot(k)

    last_tick = max(ticks)
    final = max(hops)
    hooks = {0: [send_projection, make_bias]}
    hooks[3] = [gather_projection, functools.partial(tick, 0)]
    when = {0: 3, 1: 5, 2: 7, 3: 9, 4: 11, 5: 13, 6: 15}
    when = {t: min(when.get(t, final), final) for t in range(last_tick + 1)}
    for t in range(1, last_tick + 1):
        hooks.setdefault(when[t], []).append(functools.partial(tick, t))
    late = []
    for t in range(last_tick + 1):
        if when[t] + 2 <= final:
            hooks.setdefault(when[t] + 2, []).append(functools.partial(settle, t))
        else:
            late.append(functools.partial(settle, t))

    for hook in hooks.get(0, []):
        hook()
    g_q[pl.ds(pl.multiple_of(z * qr, 16), qr), :] = qpk[...]
    g_v[pl.ds(pl.multiple_of(z * vr, 16), vr), :] = vpk[...]
    for s in range(1, final + 1):
        ways, forward = ring_ways(s)
        ring_step(phase_two, s, ways, forward)
        for hook in hooks.get(s, []):
            hook()
    for hook in late:
        hook()

    half = heads * NOPE

    def nope_pair(i, carry):
        cols = pl.ds(pl.multiple_of(i * 2 * NOPE, 2 * NOPE), 2 * NOPE)
        two = jnp.dot(ql[...], g_q[:, cols], preferred_element_type=F32).astype(BF16)
        keys = g_k[:, cols]
        for e in range(2):
            absorbed = nt_dot(two[:, e * NOPE : (e + 1) * NOPE], keys[:, e * NOPE : (e + 1) * NOPE])
            at = pl.ds(pl.multiple_of((2 * i + e) * rows, rows), rows)
            qb[at, 0:KVL] = absorbed.astype(BF16)
        cols = pl.ds(pl.multiple_of(half + i * 2 * ROPE, 2 * ROPE), 2 * ROPE)
        two = jnp.dot(ql[...], g_q[:, cols], preferred_element_type=F32).astype(BF16)
        turned = rope(two.astype(F32))
        low = lax.broadcasted_iota(jnp.int32, turned.shape, 1) < ROPE
        for e in range(2):
            kept = jnp.where(low, turned, 0.0) if e == 0 else jnp.where(low, 0.0, turned)
            at = pl.ds(pl.multiple_of((2 * i + e) * rows, rows), rows)
            qb[at, KVL : KVL + LANES] = kept.astype(BF16)
        return carry

    lax.fori_loop(0, heads // 2, nope_pair, 0)

    scale = (NOPE + ROPE) ** (-0.5)
    keys_total = (back + 1) * rows

    def one_head(h, carry):
        at = pl.ds(pl.multiple_of(h * rows, rows), rows)
        q = qb[at, :]
        top = jnp.full((rows, LANES), -jnp.inf, F32)
        for first_key in range(0, keys_total, 512):
            size = min(512, keys_total - first_key)
            s = jnp.dot(q, kbt[:, first_key : first_key + size], preferred_element_type=F32)
            s = s * scale + bias[:, first_key : first_key + size]
            s_buf[:, first_key : first_key + size] = s
            for t in range(size // LANES):
                top = jnp.maximum(top, s[:, t * LANES : (t + 1) * LANES])
        top = jnp.max(top, axis=1, keepdims=True)
        summed = jnp.zeros((rows, LANES), F32)
        mixed = jnp.zeros((rows, KVL), F32)
        for first_key in range(0, keys_total, 512):
            size = min(512, keys_total - first_key)
            p = jnp.exp(s_buf[:, first_key : first_key + size] - top)
            for t in range(size // LANES):
                summed = summed + p[:, t * LANES : (t + 1) * LANES]
            mixed = mixed + jnp.dot(
                p.astype(BF16), kb[first_key : first_key + size, 0:KVL],
                preferred_element_type=F32,
            )
        sums = jnp.sum(summed, axis=1, keepdims=True)
        mixed = (mixed / sums).astype(BF16)
        cols = pl.ds(pl.multiple_of(h * VDIM, VDIM), VDIM)
        out[:, cols] = jnp.dot(mixed, g_v[:, cols], preferred_element_type=F32).astype(BF16)
        return carry

    lax.fori_loop(0, heads, one_head, 0)

    ring_finish(phase_two)
    several = p_all.at[pl.ds(0, plane - 1)]
    pltpu.make_async_copy(several, several, p_send).wait()
    for k in range(1, back + 1):
        z_copy(k - parents[k], parents[k]).wait_send()
        pltpu.make_async_copy(x_bytes(k), x_bytes(k), x_send.at[k]).wait()


def local(mesh, hidden, segment_ids, attn_gain, down_weight, q_gain, kv_gain, q_up, key_up, value_up):
    n, n_head, n_sub = mesh.shape["seq"], mesh.shape["head"], mesh.shape["sub"]
    plane = n_head * n_sub
    rows, width = hidden.shape
    feat, cols = down_weight.shape
    main = cols // LANES * LANES
    tail = cols - main
    heads = q_up.shape[1] // (NOPE + ROPE)
    back = -(-(LONGEST - 1) // rows)

    z = lax.axis_index("seq")
    positions = z * rows + jnp.arange(rows, dtype=jnp.int32)
    half = ROPE // 2
    frequency = ROPE_BASE ** (-jnp.arange(half, dtype=F32) / half)
    angles = positions.astype(F32)[:, None] * frequency[None, :]
    cosine, sine = jnp.cos(angles), jnp.sin(angles)
    cosine = jnp.concatenate([cosine] * 4, axis=1)
    sine = jnp.concatenate([-sine, sine, -sine, sine], axis=1)
    own = lax.dynamic_slice_in_dim(segment_ids, z * rows, rows, 0)
    first = jnp.sum((segment_ids[None, :] < own[:, None]).astype(jnp.int32), axis=1, keepdims=True)

    tails = jnp.pad(down_weight[:, main:].T, ((0, 16 - tail), (0, main - feat)))
    dpk = jnp.concatenate([down_weight[:, :main], tails], axis=0)
    by_head = q_up.reshape(q_up.shape[0], heads, NOPE + ROPE)
    qpk = jnp.concatenate(
        [by_head[:, :, :NOPE].reshape(-1, heads * NOPE), by_head[:, :, NOPE:].reshape(-1, heads * ROPE)],
        axis=1,
    )
    kpk = key_up.T
    cfg = dict(
        n=n, n_sub=n_sub, plane=plane, rows=rows, feat=feat, main=main, tail=tail,
        back=back, heads=heads, gcd=math.gcd(feat, LANES),
    )
    window = (back + 1) * rows
    n_chunks = (dpk.shape[0] // 48 if dpk.shape[0] % 48 == 0 else 1) + 5
    vmem = pltpu.VMEM
    scratch = [
        vmem((n, rows, 2 * LANES), BF16),
        vmem((n * dpk.shape[0], main), BF16),
        vmem((QL, qpk.shape[1]), BF16),
        vmem((KVL, kpk.shape[1]), BF16),
        vmem((KVL, value_up.shape[1]), BF16),
        vmem((plane, rows, main + LANES), BF16),
        vmem((rows, plane * main + LANES), F32),
        vmem((window, KVL + LANES), BF16),
        vmem((KVL + LANES, window), BF16),
        vmem((heads * rows, KVL + LANES), BF16),
        vmem((rows, window), F32),
        vmem((rows, QL), BF16),
        vmem((16, LANES), BF16),
        vmem((rows, window), F32),
        vmem((rows, main), F32),
        vmem((rows, 16), F32),
        vmem((rows, LANES), F32),
        vmem((8, LANES), F32),
        pltpu.SemaphoreType.DMA((n_chunks, 2)),
        pltpu.SemaphoreType.DMA((n_chunks, 2, n // 2)),
        pltpu.SemaphoreType.DMA,
        pltpu.SemaphoreType.DMA,
        pltpu.SemaphoreType.DMA((back + 1,)),
        pltpu.SemaphoreType.DMA((back + 1,)),
        pltpu.SemaphoreType.DMA((back + 1,)),
        pltpu.SemaphoreType.DMA((back + 1,)),
    ]
    return pl.pallas_call(
        functools.partial(kernel, cfg),
        out_shape=jax.ShapeDtypeStruct((rows, heads * VDIM), BF16),
        in_specs=[pl.BlockSpec(memory_space=pltpu.VMEM)] * 11,
        out_specs=pl.BlockSpec(memory_space=pltpu.VMEM),
        scratch_shapes=scratch,
        compiler_params=pltpu.CompilerParams(
            collective_id=0, has_side_effects=True, vmem_limit_bytes=60 * 1024 * 1024
        ),
    )(
        hidden, attn_gain[None, :], dpk, qpk, kpk, value_up, q_gain[None, :], kv_gain[None, :],
        cosine, sine, first,
    )


def solution(mesh):
    placed = (
        P(("groups", "seq"), None),
        P("groups"),
        P(),
        P("seq", ("head", "sub")),
        P(),
        P(),
        P("seq", ("head", "sub")),
        P(("head", "sub"), "seq"),
        P("seq", ("head", "sub")),
    )
    return jax.shard_map(
        functools.partial(local, mesh),
        mesh=mesh,
        in_specs=placed,
        out_specs=P(("groups", "seq"), ("head", "sub")),
        check_vma=False,
    )
```

time: 859 us -> 212 us (0.25)
  the two profiles are of different devices: /device:TPU:1952 before, /device:TPU:33 now
where the time goes in v1:
time: 212 us; the launch traced here: 211 us
  Pallas kernels  200 us (94%)
  local copies, waits for them, and re-layouts  7.43 us (4%)
  other arithmetic  3.56 us (2%)
    pallas_call x1, Pallas kernels, local(): pl.pallas_call(functools.partial(kernel, cfg), out_shape=jax.ShapeDtypeSt...  200 us

profile of v1, /device:TPU:33, one launch (start us, length us, event | category | flops | bytes accessed | tf_op | source)
XLA Modules:
  0.0 211.4 jit_solution(5141919292367576776)
XLA Ops:
  0.0 0.8 dynamic_slice.3
  0.8 1.1 convert_reduce_fusion
  1.9 0.7 slice_bitcast_fusion
  2.6 1.3 broadcast_in_dim.17.q_gain
  3.8 0.7 copy.16.first
  4.6 0.9 slice.12
  5.5 0.1 copy.17
  5.6 0.7 fusion.1.dpk
  6.3 0.3 fusion.2
  6.6 0.8 pad_maximum_fusion.1
  7.4 1.1 reshape.22
  8.6 0.1 reshape.24
  8.7 0.7 pad_maximum_fusion.qpk
  9.4 200.3 %shard_map.91 = bf16[128,1024]{1,0:T(8,128)(2,1)} custom-call(bf16[128,7168]{1,0:T(8,128)(2,1)} %hid.1, f32[1,7168]{1,0:T(1,128)} %bitcast.13, bf16[240,256]{1,0:T(8,128)(2,1)} %fusion.1.dpk, bf16[48,1536]{1,0:T(8,128)(2,1)} %pad_maximum_fusion.qpk, bf16[16,1024]{1,0:T(8,128)(2,1)} %bitcast.12, bf16[16,1024]{1,0:T(8,128)(2,1)} %vpk.1, ...), custom_call_target="tpu_custom_call" | custom-call | tf_op jit(solution)/shard_map/pallas_call | solution.py:440
  209.7 1.7 copy.22
  (5 shorter events, 0.0 us)

commit v2 on v1

v2 whole, which is shorter than its diff:
```python
import functools
import math

import jax
import jax.numpy as jnp
import numpy as np
from jax import lax
from jax.experimental import pallas as pl
from jax.experimental.pallas import tpu as pltpu
from jax.sharding import PartitionSpec as P

QL = 1536
KVL = 512
ROPE = 64
NOPE = 128
VDIM = 128
LONGEST = 2048
LANES = 128
EPSILON = 1e-06
ROPE_BASE = 10000.0
BF16 = jnp.bfloat16
F32 = jnp.float32
MESH = pl.DeviceIdType.MESH


def nt_dot(a, b):
    return lax.dot_general(a, b, (((1,), (1,)), ((), ())), preferred_element_type=F32)


def kernel(
    cfg,
    hid, gain, segs, dw, qw, kw, vw, q_gain, kv_gain, freq,
    out,
    sc, g_d, g_t, g_q, g_kv, p_all, p_key, down, kd, mine, kb, kbt, qb, bias, ql, s_buf,
    acc, acc_tail, sumsq, cosine, sine, tails, turn,
    send_sem, recv_sem, y_send, y_recv, p_sem, k_sem, z_send, z_recv, x_send, x_recv,
):
    n, n_head, n_sub, plane = cfg["n"], cfg["n_head"], cfg["n_sub"], cfg["plane"]
    rows, feat, main, tail = cfg["rows"], cfg["feat"], cfg["main"], cfg["tail"]
    back, heads = cfg["back"], cfg["heads"]
    share = rows // plane
    wide = main + LANES
    z, head, sub = lax.axis_index("seq"), lax.axis_index("head"), lax.axis_index("sub")
    me = head * n_sub + sub
    group = lax.axis_index("groups")
    parity = lax.rem(group, 2)
    pair = {"groups": group + 1 - 2 * parity}

    def peer(d):
        other = lax.rem(me + d, plane)
        return {"head": other // n_sub, "sub": lax.rem(other, n_sub)}

    def along(d):
        return {"seq": lax.rem(z + d + n, n)}

    sibling = {"sub": 1 - sub}

    def column(d):
        return {"head": lax.rem(head + d, n_head)}

    jumps = sorted({1, n - 1, 4, n - 4})
    barrier = pltpu.get_barrier_semaphore()
    for d in jumps:
        pl.semaphore_signal(barrier, inc=1, device_id=along(d), device_id_type=MESH)
    for d in range(1, plane):
        pl.semaphore_signal(barrier, inc=1, device_id=peer(d), device_id_type=MESH)
    pl.semaphore_signal(barrier, inc=1, device_id=pair, device_id_type=MESH)
    pl.semaphore_wait(barrier, len(jumps) + plane)

    dr, qr, kr = feat, qw.shape[0], kw.shape[0]
    common, half_rows = cfg["d_common"], (feat - cfg["d_common"]) // 2
    q_third = qr // 3

    def rows_of(src, held, size, offset, length, lanes=None):
        def own(par):
            at = pl.ds(offset(par), length)
            return src.at[at, pl.ds(0, lanes)] if lanes else src.at[at, :]

        def there(o, par):
            return held.at[pl.ds(pl.multiple_of(o * size + offset(par), 16), length), :]

        return own, there

    def fixed(offset):
        return lambda par: offset

    def kv_there(o, par):
        return g_kv.at[pl.ds(pl.multiple_of(par * KVL + o * kr, 16), kr), :]

    chunks = [
        rows_of(dw, g_d, dr, lambda par: pl.multiple_of(common + par * half_rows, 16), half_rows, main),
        rows_of(dw, g_d, dr, fixed(0), common // 2, main),
        rows_of(dw, g_d, dr, fixed(common // 2), common // 2, main),
        rows_of(tails, g_t, 16, fixed(0), 16),
        (None, kv_there),
        rows_of(qw, g_q, qr, lambda par: pl.multiple_of(q_third * (1 + par), 16), q_third),
        rows_of(qw, g_q, qr, fixed(0), q_third),
    ]
    D_SHARED, TAIL, KV, Q_SHARED = 0, 3, 4, 5
    shared = {D_SHARED: 0, KV: 1, Q_SHARED: 2}
    phase_one, phase_two = [0, 1, 2, 3, 4], [5, 6]
    hops = (n - 1 - n // 2, n // 2)
    signs = (1, -1)

    def ring_copy(c, way, step_index, origin, src=None):
        there = chunks[c][1](origin, parity)
        return pltpu.make_async_remote_copy(
            src_ref=there if src is None else src,
            dst_ref=there,
            send_sem=send_sem.at[c, way],
            recv_sem=recv_sem.at[c, way, step_index],
            device_id=along(signs[way]),
            device_id_type=MESH,
        )

    def pair_copy(c, way, step_index, origin, par):
        there = chunks[c][1](origin, par)
        return pltpu.make_async_remote_copy(
            src_ref=there,
            dst_ref=there,
            send_sem=y_send.at[shared[c], way],
            recv_sem=y_recv.at[shared[c], way, step_index],
            device_id=pair,
            device_id_type=MESH,
        )

    def origin_of(way, s):
        return lax.rem(z - signs[way] * s + 2 * n, n)

    def ring_start(which):
        for c in which:
            for way in (0, 1):
                if c == KV:
                    for par, src in enumerate((kw, vw)):
                        @pl.when(parity == par)
                        def _():
                            ring_copy(c, way, 0, z, src=src).start()
                else:
                    ring_copy(c, way, 0, z, src=chunks[c][0](parity)).start()

    def ring_step(which, s, first=False):
        static = isinstance(s, int)
        for c in which:
            for way in (0, 1):
                if static and s > hops[way]:
                    continue
                origin = origin_of(way, s)
                copy = ring_copy(c, way, s - 1, origin)
                copy.wait_recv()
                if not static or s < hops[way]:
                    copy.wait_send()
                    ring_copy(c, way, s, origin).start()
                if c in shared:
                    if not first:
                        pair_copy(c, way, s - 1, origin, parity).wait_send()
                    pair_copy(c, way, s - 1, origin, parity).start()

    def pair_wait(c, s):
        for way in (0, 1):
            if not isinstance(s, int) or s <= hops[way]:
                pair_copy(c, way, s - 1, origin_of(way, s), 1 - parity).wait_recv()

    def ring_finish(which):
        for c in which:
            for way in (0, 1):
                ring_copy(c, way, hops[way] - 1, z).wait_send()
                if c in shared:
                    pair_copy(c, way, hops[way] - 1, z, parity).wait_send()

    ring_start([c for c in phase_one if c != TAIL])

    turn[...] = jnp.zeros_like(turn)
    turn[0:feat, 0:tail] = dw[:, main : main + tail].astype(F32)
    for t in range(main // LANES):
        flat = turn[t * LANES : (t + 1) * LANES, :].T
        tails[:, t * LANES : (t + 1) * LANES] = flat[0:16, :].astype(BF16)

    lane = lax.broadcasted_iota(jnp.int32, (rows, 2 * LANES), 1)
    period = LANES // math.gcd(feat, LANES)
    per_group = period * feat // LANES

    def cut(g, sq):
        tiles = []
        for t in range(per_group):
            at = pl.ds(pl.multiple_of((g * per_group + t) * LANES, LANES), LANES)
            tile = hid[:, at].astype(F32)
            sq = sq + tile * tile
            tiles.append(tile * gain[pl.ds(g * per_group + t, 1), :])
        for i in range(period):
            low, shift = i * feat // LANES, i * feat % LANES
            high = -(-(i * feat + feat) // LANES)
            part = jnp.concatenate(tiles[low:high], axis=1)
            if shift:
                part = pltpu.roll(part, part.shape[1] - shift, axis=1)
            kept = jnp.where(lane < feat, part[:, : 2 * LANES], 0.0)
            sc[g * period + i] = kept.astype(BF16)
        return sq

    sumsq[...] = lax.fori_loop(0, n // period, cut, jnp.zeros((rows, LANES), F32))
    ring_start([TAIL])

    acc[...] = jnp.zeros_like(acc)
    acc_tail[...] = jnp.zeros_like(acc_tail)

    def project(origin, own=False):
        lhs = sc[origin]
        if own:
            rhs, last = dw[:, 0:main], tails[...]
        else:
            rhs = g_d[pl.ds(pl.multiple_of(origin * feat, 16), feat), :]
            last = g_t[pl.ds(pl.multiple_of(origin * 16, 16), 16), :]
        acc[...] += jnp.dot(lhs[:, :feat], rhs, preferred_element_type=F32)
        acc_tail[...] += nt_dot(lhs, last)

    def project_step(s):
        pair_wait(D_SHARED, s)
        for way in (0, 1):
            if not isinstance(s, int) or s <= hops[way]:
                project(origin_of(way, s))

    def unit(k):
        return kb.at[pl.ds(pl.multiple_of(k * rows + me * share, 16), share), :]

    def peer_index(d):
        return lax.rem(head + d, n_head) * n_sub + sub

    P_COL, P_SIB, P_COL_OUT, P_SIB_OUT = 0, 1, 2, 3

    def p_copy(j, device, out_sem, in_sem):
        return pltpu.make_async_remote_copy(
            src_ref=p_all.at[j], dst_ref=p_all.at[j],
            send_sem=p_sem.at[out_sem], recv_sem=p_sem.at[in_sem],
            device_id=device, device_id_type=MESH,
        )

    def k_copy(d):
        other = lax.rem(me + d, plane)
        return pltpu.make_async_remote_copy(
            src_ref=p_all.at[me, pl.ds(pl.multiple_of(other * share, 16), share), :],
            dst_ref=p_key.at[me],
            send_sem=k_sem.at[0], recv_sem=k_sem.at[1],
            device_id=peer(d), device_id_type=MESH,
        )

    def wait_bytes(ref, sem):
        pltpu.make_async_copy(ref, ref, sem).wait()

    def send_projection():
        mean = jnp.sum(sumsq[...], axis=1, keepdims=True) / (n * feat)
        inverse = lax.rsqrt(mean + EPSILON)
        p_all[me, :, 0:main] = (acc[...] * inverse).astype(BF16)
        p_all[me, :, main:wide] = jnp.zeros((rows, LANES), BF16)
        p_all[me, :, main : main + 16] = (acc_tail[...] * inverse).astype(BF16)
        for d in range(1, plane):
            k_copy(d).start()
        for d in range(1, n_head):
            p_copy(me, column(d), P_COL_OUT, P_COL).start()
        p_copy(me, sibling, P_SIB_OUT, P_SIB).start()
        p_key[me] = p_all[me, pl.ds(pl.multiple_of(me * share, 16), share), :]

    def relay_projection():
        wait_bytes(p_all.at[pl.ds(0, n_head - 1)], p_sem.at[P_COL])
        for d in range(1, n_head):
            p_copy(peer_index(d), sibling, P_SIB_OUT, P_SIB).start()

    def rope(values, cos, sin):
        w = values.shape[1]
        at = lax.broadcasted_iota(jnp.int32, values.shape, 1)
        swapped = jnp.where(
            lax.rem(at, ROPE) < ROPE // 2,
            pltpu.roll(values, w - ROPE // 2, axis=1),
            pltpu.roll(values, ROPE // 2, axis=1),
        )
        return values * cos + swapped * sin

    def normed(values, gains):
        scale = lax.rsqrt(jnp.mean(values * values, axis=1, keepdims=True) + EPSILON)
        parts = []
        for t in range(values.shape[1] // LANES):
            part = values[:, t * LANES : (t + 1) * LANES]
            parts.append((part * scale * gains[t : t + 1, :]).astype(BF16))
        return parts

    def write_keys(target, columns, cos, sin):
        count = columns.shape[0]
        for t, part in enumerate(normed(columns[:, 0:KVL], kv_gain)):
            target[0:count, t * LANES : (t + 1) * LANES] = part
        turned = rope(columns[:, KVL : KVL + LANES], cos, sin)
        turned = turned + pltpu.roll(turned, ROPE, axis=1)
        target[0:count, KVL : KVL + LANES] = turned.astype(BF16)

    first_key = QL // (main + tail)
    key_lane = QL - first_key * main

    def key_share():
        wait_bytes(p_key.at[pl.ds(0, plane - 1)], k_sem.at[1])
        kd[...] = jnp.zeros_like(kd)
        for j in range(first_key, plane):
            piece = pltpu.roll(p_key[j].astype(F32), j * tail, axis=1)
            low = (j - first_key) * main
            kd[:, low : low + wide] += piece
        at = pl.ds(pl.multiple_of(me * share, 16), share)
        write_keys(mine, kd[:, key_lane : key_lane + KVL + LANES], cosine[at, :], sine[at, :])

    def tables():
        position = z * rows + lax.broadcasted_iota(jnp.int32, (rows, LANES), 0)
        angles = position.astype(F32) * freq[...]
        at = lax.broadcasted_iota(jnp.int32, (rows, LANES), 1)
        cosine[...] = jnp.cos(angles)
        sine[...] = jnp.where(lax.rem(at, ROPE) < ROPE // 2, -1.0, 1.0) * jnp.sin(angles)

    def make_bias():
        query_pos = z * rows + lax.broadcasted_iota(jnp.int32, (rows, rows), 0)
        own = jnp.broadcast_to(segs[pl.ds(z, 1), :], (rows, rows)).T
        for k in range(back + 1):
            key_pos = (z - k) * rows + lax.broadcasted_iota(jnp.int32, (rows, rows), 1)
            seg = segs[pl.ds(lax.rem(z - k + 2 * n, n), 1), :]
            allowed = (key_pos <= query_pos) & (key_pos >= 0) & (seg == own)
            bias[:, k * rows : (k + 1) * rows] = jnp.where(allowed, 0.0, -jnp.inf)

    def gather_projection():
        wait_bytes(p_all.at[pl.ds(0, n_head)], p_sem.at[P_SIB])
        down[...] = jnp.zeros_like(down)
        for j in range(plane):
            piece = p_all[j].astype(F32)
            if j:
                piece = pltpu.roll(piece, j * tail, axis=1)
            down[:, j * main : j * main + wide] += piece
        for t, part in enumerate(normed(down[:, 0:QL], q_gain)):
            ql[:, t * LANES : (t + 1) * LANES] = part
        write_keys(kb, down[:, QL : QL + KVL + LANES], cosine[...], sine[...])

    def z_copy(k, jump):
        return pltpu.make_async_remote_copy(
            src_ref=unit(k) if k else mine, dst_ref=unit(k + jump),
            send_sem=z_send.at[k + jump], recv_sem=z_recv.at[k + jump],
            device_id=along(jump), device_id_type=MESH,
        )

    def x_copy(k, j, device, out_sem, in_sem):
        ref = kb.at[pl.ds(pl.multiple_of(k * rows + j * share, 16), share), :]
        return pltpu.make_async_remote_copy(
            src_ref=ref, dst_ref=ref, send_sem=x_send.at[out_sem, k], recv_sem=x_recv.at[in_sem, k],
            device_id=device, device_id_type=MESH,
        )

    parents, ticks = {}, {0: [0]}
    for k in range(1, back + 1):
        parents[k] = 1 if k % 4 else 4
        ticks.setdefault(k // 4 + k % 4, []).append(k)

    def x_bytes(k, units):
        return kb.at[pl.ds(k * rows, units * share), :]

    def transpose_slot(k):
        for t in range(kb.shape[1] // LANES):
            tile = kb[k * rows : (k + 1) * rows, t * LANES : (t + 1) * LANES]
            kbt[t * LANES : (t + 1) * LANES, k * rows : (k + 1) * rows] = (
                tile.astype(F32).T.astype(BF16)
            )

    def tick(t):
        arrived = sorted(ticks[t], key=lambda k: k % 4)
        for k in arrived:
            if k:
                z_copy(k - parents[k], parents[k]).wait_recv()
            for jump in (4, 1):
                if k + jump <= back and parents[k + jump] == jump:
                    if jump == 4 and k % 4:
                        continue
                    z_copy(k, jump).start()
        for k in arrived:
            if k:
                for d in range(1, n_head):
                    x_copy(k, me, column(d), 0, 0).start()
                x_copy(k, me, sibling, 1, 1).start()

    def relay(t):
        for k in ticks[t]:
            if k:
                wait_bytes(x_bytes(k, n_head - 1), x_recv.at[0, k])
                for d in range(1, n_head):
                    x_copy(k, peer_index(d), sibling, 1, 1).start()

    def settle(t):
        for k in ticks[t]:
            if k:
                wait_bytes(x_bytes(k, n_head), x_recv.at[1, k])
            transpose_slot(k)

    project(z, own=True)
    tables()
    q_start = min(cfg["q_start"], max(hops))
    last_d, final = max(hops), q_start + max(hops)
    ring_step(phase_one, 1, first=True)

    def one_step(s, carry):
        ring_step(phase_one, s)
        project_step(s - 1)
        return carry

    lax.fori_loop(2, min(q_start, min(hops)), one_step, 0)
    for par, src in enumerate((kw, vw)):
        g_kv[pl.ds(pl.multiple_of(par * KVL + z * kr, 16), kr), :] = src[...]
    g_q[pl.ds(pl.multiple_of(z * qr, 16), qr), :] = qw[...]

    hooks = {}

    def at_tick(when, what, *args):
        hooks.setdefault(min(when, final), []).append(functools.partial(what, *args))

    base = last_d
    at_tick(base, send_projection)
    at_tick(base, make_bias)
    at_tick(base + 1, key_share)
    at_tick(base + 1, tick, 0)
    at_tick(base + 2, relay_projection)
    for t, when in enumerate(cfg["when"], start=1):
        at_tick(base + when, tick, t)
    for t, when in enumerate(cfg["relay"], start=1):
        at_tick(base + when, relay, t)
    at_tick(base + 5, gather_projection)
    at_tick(base + 6, settle, 0)
    for t, when in enumerate(cfg["settle"], start=1):
        at_tick(base + when, settle, t)

    for step in range(min(q_start, min(hops)), final + 1):
        if step <= last_d:
            ring_step(phase_one, step)
        if step == q_start:
            ring_start(phase_two)
        elif step > q_start:
            ring_step(phase_two, step - q_start, first=step == q_start + 1)
        if step <= last_d:
            project_step(step - 1)
        if step == last_d:
            project_step(step)
        for hook in hooks.get(step, []):
            hook()

    def collect(s, carry):
        pair_wait(KV, s)
        pair_wait(Q_SHARED, s)
        return carry

    lax.fori_loop(1, min(hops) + 1, collect, 0)
    pair_wait(KV, max(hops))
    pair_wait(Q_SHARED, max(hops))

    low = lax.broadcasted_iota(jnp.int32, (rows, LANES), 1) < ROPE

    def query_pair(i, carry):
        width = 2 * (NOPE + ROPE)
        cols = pl.ds(pl.multiple_of(i * width, width), width)
        two = jnp.dot(ql[...], g_q[:, cols], preferred_element_type=F32).astype(BF16).astype(F32)
        one, middle, end = two[:, 0:LANES], two[:, LANES : 2 * LANES], two[:, 2 * LANES :]
        other = jnp.where(low, pltpu.roll(middle, ROPE, axis=1), pltpu.roll(end, ROPE, axis=1))
        turned = rope(jnp.where(low, middle, end), cosine[...], sine[...])
        for e, nope in enumerate((one, other)):
            lanes = pl.ds(pl.multiple_of((2 * i + e) * NOPE, NOPE), NOPE)
            absorbed = nt_dot(nope.astype(BF16), g_kv[0:KVL, lanes])
            at = pl.ds(pl.multiple_of((2 * i + e) * rows, rows), rows)
            qb[at, 0:KVL] = absorbed.astype(BF16)
            kept = jnp.where(low, turned, 0.0) if e == 0 else jnp.where(low, 0.0, turned)
            qb[at, KVL : KVL + LANES] = kept.astype(BF16)
        return carry

    lax.fori_loop(0, heads // 2, query_pair, 0)

    scale = (NOPE + ROPE) ** (-0.5)
    keys_total = (back + 1) * rows

    def one_head(h, carry):
        at = pl.ds(pl.multiple_of(h * rows, rows), rows)
        q = qb[at, :]
        top = jnp.full((rows, LANES), -jnp.inf, F32)
        for first_key in range(0, keys_total, 512):
            size = min(512, keys_total - first_key)
            s = jnp.dot(q, kbt[:, first_key : first_key + size], preferred_element_type=F32)
            s = s * scale + bias[:, first_key : first_key + size]
            s_buf[:, first_key : first_key + size] = s
            for t in range(size // LANES):
                top = jnp.maximum(top, s[:, t * LANES : (t + 1) * LANES])
        top = jnp.max(top, axis=1, keepdims=True)
        summed = jnp.zeros((rows, LANES), F32)
        mixed = jnp.zeros((rows, KVL), F32)
        for first_key in range(0, keys_total, 512):
            size = min(512, keys_total - first_key)
            p = jnp.exp(s_buf[:, first_key : first_key + size] - top)
            for t in range(size // LANES):
                summed = summed + p[:, t * LANES : (t + 1) * LANES]
            mixed = mixed + jnp.dot(
                p.astype(BF16), kb[first_key : first_key + size, 0:KVL],
                preferred_element_type=F32,
            )
        sums = jnp.sum(summed, axis=1, keepdims=True)
        mixed = (mixed / sums).astype(BF16)
        cols = pl.ds(pl.multiple_of(h * VDIM, VDIM), VDIM)
        out[:, cols] = jnp.dot(mixed, g_kv[KVL : 2 * KVL, cols], preferred_element_type=F32).astype(BF16)
        return carry

    lax.fori_loop(0, heads, one_head, 0)

    ring_finish(phase_one)
    ring_finish(phase_two)
    wait_bytes(p_all.at[pl.ds(0, n_head - 1)], p_sem.at[P_COL_OUT])
    wait_bytes(p_all.at[pl.ds(0, n_head)], p_sem.at[P_SIB_OUT])
    wait_bytes(p_key.at[pl.ds(0, plane - 1)], k_sem.at[0])
    for k in range(1, back + 1):
        z_copy(k - parents[k], parents[k]).wait_send()
        wait_bytes(x_bytes(k, n_head - 1), x_send.at[0, k])
        wait_bytes(x_bytes(k, n_head), x_send.at[1, k])


def local(mesh, hidden, segment_ids, attn_gain, down_weight, q_gain, kv_gain, q_up, key_up, value_up):
    n, n_head, n_sub = mesh.shape["seq"], mesh.shape["head"], mesh.shape["sub"]
    plane = n_head * n_sub
    rows = hidden.shape[0]
    feat, cols = down_weight.shape
    main = cols // LANES * LANES
    heads = q_up.shape[1] // (NOPE + ROPE)
    back = -(-(LONGEST - 1) // rows)
    half = ROPE // 2
    exponent = -np.arange(half, dtype=np.float32) / np.float32(half)
    freq = np.tile(np.float32(ROPE_BASE) ** exponent, LANES // half)[None, :]
    cfg = dict(
        n=n, n_head=n_head, n_sub=n_sub, plane=plane, rows=rows, feat=feat, main=main,
        tail=cols - main, back=back, heads=heads, d_common=96, q_start=11,
        when=(3, 5, 7, 9, 10, 11), relay=(4, 6, 8, 10, 11, 12), settle=(5, 7, 9, 11, 12, 13),
    )
    window = (back + 1) * rows
    n_chunks, reach = 7, n // 2
    vmem, dma = pltpu.VMEM, pltpu.SemaphoreType.DMA
    scratch = [
        vmem((n, rows, 2 * LANES), BF16),
        vmem((n * feat, main), BF16),
        vmem((n * 16, main), BF16),
        vmem(q_up.shape[:0] + (QL, q_up.shape[1]), BF16),
        vmem((2 * KVL, value_up.shape[1]), BF16),
        vmem((plane, rows, main + LANES), BF16),
        vmem((plane, rows // plane, main + LANES), BF16),
        vmem((rows, plane * main + LANES), F32),
        vmem((rows // plane, (plane - QL // cols) * main + LANES), F32),
        vmem((rows // plane, KVL + LANES), BF16),
        vmem((window, KVL + LANES), BF16),
        vmem((KVL + LANES, window), BF16),
        vmem((heads * rows, KVL + LANES), BF16),
        vmem((rows, window), F32),
        vmem((rows, QL), BF16),
        vmem((rows, window), F32),
        vmem((rows, main), F32),
        vmem((rows, 16), F32),
        vmem((rows, LANES), F32),
        vmem((rows, LANES), F32),
        vmem((rows, LANES), F32),
        vmem((16, main), BF16),
        vmem((main, LANES), F32),
        dma((n_chunks, 2)),
        dma((n_chunks, 2, reach)),
        dma((3, 2)),
        dma((3, 2, reach)),
        dma((4,)),
        dma((2,)),
        dma((back + 1,)),
        dma((back + 1,)),
        dma((2, back + 1)),
        dma((2, back + 1)),
    ]
    return pl.pallas_call(
        functools.partial(kernel, cfg),
        out_shape=jax.ShapeDtypeStruct((rows, heads * VDIM), BF16),
        in_specs=[pl.BlockSpec(memory_space=pltpu.VMEM)] * 10,
        out_specs=pl.BlockSpec(memory_space=pltpu.VMEM),
        scratch_shapes=scratch,
        compiler_params=pltpu.CompilerParams(
            collective_id=0, has_side_effects=True, vmem_limit_bytes=60 * 1024 * 1024
        ),
    )(
        hidden, attn_gain.reshape(-1, LANES), segment_ids.reshape(n, rows), down_weight, q_up, key_up.T,
        value_up, q_gain.reshape(-1, LANES), kv_gain.reshape(-1, LANES), jnp.asarray(freq),
    )


def solution(mesh):
    placed = (
        P(("groups", "seq"), None),
        P("groups"),
        P(),
        P("seq", ("head", "sub")),
        P(),
        P(),
        P("seq", ("head", "sub")),
        P(("head", "sub"), "seq"),
        P("seq", ("head", "sub")),
    )
    return jax.shard_map(
        functools.partial(local, mesh),
        mesh=mesh,
        in_specs=placed,
        out_specs=P(("groups", "seq"), ("head", "sub")),
        check_vma=False,
    )
```

time: 212 us -> 182 us (0.86)
  Pallas kernels: 200 us -> 178 us
  local copies, waits for them, and re-layouts: 7.43 us -> 3.37 us
  other arithmetic: 3.56 us -> 0 us
    pallas_call x1, Pallas kernels: 200 us -> 178 us  [local(): pl.pallas_call(functools.partial(kernel, cfg), out_shape=jax.ShapeDtypeSt...]
    concatenate x3 -> x0, other arithmetic: 2.17 us -> none  [the longest x1 0.83 us: local(): cosine = jnp.concatenate([cosine] * 4, axis=1)]
where the time goes in v2:
time: 182 us
  Pallas kernels  178 us (98%)
  local copies, waits for them, and re-layouts  3.37 us (2%)
    pallas_call x1, Pallas kernels, local(): pl.pallas_call(functools.partial(kernel, cfg), out_shape=jax.ShapeDtypeSt...  178 us

profile of v2, /device:TPU:33, one launch (start us, length us, event | category | flops | bytes accessed | tf_op | source)
XLA Modules:
  0.0 181.5 jit_solution(15358200489599517584)
XLA Ops:
  0.0 1.7 copy.11.dw
  1.7 178.1 %shard_map.100 = bf16[128,1024]{1,0:T(8,128)(2,1)} custom-call(bf16[128,7168]{1,0:T(8,128)(2,1)} %hid.1, f32[56,128]{1,0:T(8,128)} %bitcast.6, s32[32,128]{1,0:T(8,128)} %bitcast.7, bf16[224,264]{1,0:T(8,128)(2,1)} %copy.11.dw, bf16[48,1536]{1,0:T(8,128)(2,1)} %qw.1, bf16[16,1024]{1,0:T(8,128)(2,1)} %bitcast.5, bf16[16,1024]{1,0:T(8,128)(2,1)} %vw.1, ...), custom_call_target="tpu_custom_call" | custom-call | tf_op jit(solution)/shard_map/pallas_call | solution.py:569
  179.9 1.7 copy.13
